TPU v7x, 32 devices: a whole 2x2x4 slice. The times are simulated.
32 devices in a mesh: ga: 8 (over z, x), band: 4 (over y, core).
Axes of the slice: x: 2, y: 2, z: 4, core: 2. Of those that a mesh axis runs over, the one named last changes fastest.
Arguments:
- coeffs: bfloat16 [2, 512, 40960], P(None, ('ga', 'band')), may hold values from -6 to 6
- projectors: bfloat16 [1280, 2, 40960], P(None, None, 'ga'), may hold values from -0.01953125 to 0.01953125
- block_coupling: float32 [1280, 18], replicated, may hold values from -12 to 12
- atom_counts: int32 [160], replicated, may hold values from 4 to 18, as said below
- wave_counts: int32 [8], P('ga'), may hold values from 3840 to 5120
Outputs:
- applied: bfloat16 [2, 512, 40960], P(None, ('ga', 'band'))
- band_energy: float32 [512], P(('ga', 'band'))
- total_energy: float32 [], replicated
Inputs may be any that keep to these rules, and one draw needn't show every extreme that they name: `atom_counts`: each atom has 4, 8 or 18 projectors, the counts sum to 1280 and the largest is 18.
All inputs are finite; a program needn't handle non-finite values.
Results may differ from a plain program's by a relative error of at most 0.013.
Values may be sent and summed in bfloat16 or wider, within the bound.
A program may use at most 128 MiB of HBM per device.

v0:
```python
import math

import jax
import jax.numpy as jnp
from jax import lax
from jax.sharding import PartitionSpec as P


def block_tables(atom_counts, row_ids):
    atom_ends = jnp.cumsum(atom_counts)
    atom_starts = atom_ends - atom_counts
    inside = (atom_starts[None, :] <= row_ids[:, None]) & (atom_ends[None, :] > row_ids[:, None])
    block_first = jnp.sum(jnp.where(inside, atom_starts[None, :], 0), axis=1)
    block_length = jnp.sum(jnp.where(inside, atom_counts[None, :], 0), axis=1)
    return (block_first, block_length)


def coupling_matrix(block_first, block_length, coupling_rows, column_count):
    column_ids = lax.iota(jnp.int32, column_count)
    offsets = column_ids[None, :] - block_first[:, None]
    matrix = jnp.zeros((coupling_rows.shape[0], column_count), jnp.float32)
    for offset in range(coupling_rows.shape[1]):
        hit = (offsets == offset) & (offset < block_length[:, None])
        matrix = jnp.where(hit, coupling_rows[:, offset : offset + 1], matrix)
    return matrix


def shards(coeffs, projectors, block_coupling, atom_counts, wave_counts):
    moved_bands = lax.all_to_all(coeffs, "ga", split_axis=2, concat_axis=1, tiled=True)
    own_bands = coeffs.shape[1]
    group_bands = moved_bands.shape[1]
    wave_slots = projectors.shape[2]
    proj_total_rows = projectors.shape[0]
    in_sphere = (lax.iota(jnp.int32, wave_slots) < wave_counts[0]).astype(jnp.float32)
    masked = moved_bands * in_sphere.astype(jnp.bfloat16)
    real_part = masked[0]
    imag_part = masked[1]
    stacked = jnp.concatenate(
        [jnp.concatenate([real_part, imag_part], 1), jnp.concatenate([imag_part, -real_part], 1)], 0
    )
    flat_beta = projectors.reshape(proj_total_rows, 2 * wave_slots)
    contract_last = (((1,), (1,)), ((), ()))
    contract_first = (((0,), (0,)), ((), ()))
    ga_index = lax.axis_index("ga")
    local_terms = lax.dot_general(
        flat_beta, stacked, contract_last, preferred_element_type=jnp.float32
    )
    projections = lax.psum(local_terms, "ga")
    block_first, block_length = block_tables(atom_counts, lax.iota(jnp.int32, proj_total_rows))
    matrix = coupling_matrix(block_first, block_length, block_coupling, proj_total_rows)
    coupled = jnp.dot(
        matrix, projections, precision=lax.Precision.HIGHEST, preferred_element_type=jnp.float32
    )
    energy_terms = jnp.sum(projections * coupled, axis=0)
    group_energy = (energy_terms[:group_bands] + energy_terms[group_bands:]) / proj_total_rows
    band_energy = lax.dynamic_slice_in_dim(group_energy, ga_index * own_bands, own_bands, 0)
    total_energy = lax.psum(jnp.sum(group_energy), "band")
    products = lax.dot_general(
        coupled.astype(jnp.bfloat16), flat_beta, contract_first, preferred_element_type=jnp.float32
    )
    band_total = own_bands * lax.axis_size("ga") * lax.axis_size("band")
    total_energy = total_energy / math.sqrt(band_total)
    real_out = products[:group_bands, :wave_slots] - products[group_bands:, wave_slots:]
    imag_out = products[:group_bands, wave_slots:] + products[group_bands:, :wave_slots]
    result = (jnp.stack([real_out, imag_out]) * in_sphere).astype(jnp.bfloat16)
    applied = lax.all_to_all(result, "ga", split_axis=1, concat_axis=2, tiled=True)
    return (applied, band_energy, total_energy)


def solution(mesh):
    placed = (P(None, ("ga", "band"), None), P(None, None, "ga"), P(), P(), P("ga"))
    return jax.shard_map(
        shards,
        mesh=mesh,
        in_specs=placed,
        out_specs=(P(None, ("ga", "band"), None), P(("ga", "band")), P()),
        check_vma=False,
    )
```

profile of v0, /device:TPU:0, one launch (start us, length us, event | category | flops | bytes accessed | tf_op | source)
XLA Modules:
  0.0 430.2 jit_solution(13984395675737779399)
XLA Ops:
  7.2 38.0 %copy.21 = bf16[2,16,40960]{1,0,2:T(2,128)(2,1)} copy(bf16[2,16,40960]{2,1,0:T(8,128)(2,1)} %param.5) | data formatting | bytes 5242880 | tf_op args[0]
  45.1 24.1 %reshape.129 = bf16[8,2,81920]{2,1,0:T(2,128)(2,1)} reshape(bf16[40960,2,16]{2,1,0:T(2,128)(2,1)} %bitcast.40) | data formatting | bytes 5242880
  69.2 7.3 %all-to-all-start = ((bf16[8,2,81920]{2,1,0:T(2,128)(2,1)}), bf16[8,2,81920]{2,1,0:T(2,128)(2,1)S(1)}, u32[]{:S(2)}, u32[]{:S(2)}) async-start(bf16[8,2,81920]{2,1,0:T(2,128)(2,1)} %reshape.129), calls=%async_computation | async-start | bytes 5242880 | tf_op jit(solution)/shard_map/all_to_all | solution.py:29
  76.5 0.2 all-reduce.3.cloned.1.call-start
  77.4 23.8 %copy.29 = bf16[160,8,2,5120]{3,1,2,0:T(8,128)(2,1)} copy(bf16[160,8,2,5120]{3,2,1,0:T(2,128)(2,1)} %bitcast.41) | data formatting | bytes 52428800
  101.1 34.8 %all-to-all-done = bf16[8,2,81920]{2,1,0:T(2,128)(2,1)S(1)} async-done(((bf16[8,2,81920]{2,1,0:T(2,128)(2,1)}), bf16[8,2,81920]{2,1,0:T(2,128)(2,1)S(1)}, u32[]{:S(2)}, u32[]{:S(2)}) %all-to-all-start) | async-done | bytes 2621472 | tf_op jit(solution)/shard_map/all_to_all | solution.py:29
  136.0 17.1 %reshape.130 = bf16[40960,2,16]{2,1,0:T(2,128)(2,1)} reshape(bf16[8,2,81920]{2,1,0:T(2,128)(2,1)S(1)} %all-to-all-done) | data formatting | bytes 5242880
  153.0 37.5 %copy.28 = bf16[2,16,8,5120]{3,1,2,0:T(8,128)(2,1)S(1)} copy(bf16[2,16,8,5120]{1,0,3,2:T(2,128)(2,1)} %bitcast.39) | data formatting | bytes 5242880 | tf_op jit(solution)/shard_map/all_to_all | solution.py:29
  190.5 0.3 bitcast_multiply_fusion
  190.9 0.2 slice_bitcast_fusion.1
  191.1 0.1 fusion.168
  191.2 0.0 copy-start.1
  191.2 0.0 copy-start
  191.2 28.8 %fusion.138 = f32[1280,256]{0,1:T(8,128)} fusion(bf16[1280,10240]{1,0:T(8,128)(2,1)} %bitcast.37, bf16[128,5120]{1,0:T(8,128)(2,1)S(1)} %fusion.168, bf16[128,5120]{1,0:T(8,128)(2,1)S(1)} %get-tuple-element.28, bf16[128,5120]{1,0:T(8,128)(2,1)S(1)} %get-tuple-element.27), kind=kOutput, calls=%fused_computation.122 | convolution fusion | flops 6731857920 | bytes 31457280 | tf_op jit(solution)/shard_map/dot_general | solution.py:45
  220.0 0.0 all-reduce.3.cloned.1.call-update
  220.1 0.0 copy-done.1
  220.1 0.3 reduce-window.9
  220.4 0.1 slice.88
  220.5 0.1 slice_reduce_fusion.18
  220.6 0.0 copy-done
  220.6 0.2 slice_reduce_fusion.17
  220.9 0.1 add_bitcast_fusion
  220.9 0.3 select_reduce_fusion
  221.3 81.7 %all-reduce.3.cloned.1.call-done = f32[1280,256]{0,1:T(8,128)} async-done(((f32[1280,256]{0,1:T(8,128)}), f32[1280,256]{0,1:T(8,128)}) %all-reduce.3.cloned.1.call-update) | async-done | bytes 1310736 | tf_op jit(solution)/shard_map/psum | solution.py:48
  303.0 29.8 %fusion = f32[1280,256]{1,0:T(8,128)} fusion(f32[1280,256]{0,1:T(8,128)} %all-reduce.3.cloned.1.call-done, f32[1280]{0:T(1024)S(1)} %get-tuple-element.19, f32[1280]{0:T(1024)S(1)} %get-tuple-element.20, f32[1280]{0:T(1024)S(1)} %get-tuple-element.4, f32[1280]{0:T(1024)S(1)} %get-tuple-element.5, f32[1280]{0:T(1024)S(1)} %get-tuple-element.6, ...), kind=kOutput, calls=%fused_computation | convolution fusion | flops 5123276800 | bytes 2741760 | tf_op jit(solution)/shard_map/dot_general | solution.py:51
  332.7 13.0 %fusion.144 = f32[256,10240]{1,0:T(8,128)S(1)} fusion(bf16[1280,10240]{1,0:T(8,128)(2,1)} %bitcast.38, f32[1280,256]{1,0:T(8,128)} %fusion), kind=kOutput, calls=%fused_computation.136 | convolution fusion | flops 6711214080 | bytes 38010880 | tf_op jit(solution)/shard_map/dot_general | solution.py:58
  345.8 0.8 fusion.142
  346.5 0.5 fusion.81
  347.0 4.2 copy.24
  351.2 3.7 all-to-all-start.1
  354.9 2.8 copy.26
  357.6 1.9 multiply_reduce_fusion
  359.5 0.6 fusion.169
  360.2 7.3 %psum.15 = f32[]{:T(128)} all-reduce(f32[]{:T(128)} %get-tuple-element.23), channel_id=1, replica_groups=mesh['ga'=8,'band'=4] {'band'}, use_global_device_ids=true, to_apply=%region_7.8 | all-reduce | flops 1 | bytes 8 | tf_op jit(solution)/shard_map/psum | solution.py:57
  367.5 0.6 dynamic_slice.3
  368.7 45.7 %all-to-all-done.1 = bf16[2,128,5120]{2,0,1:T(2,128)(2,1)S(1)} async-done(((bf16[2,128,5120]{2,0,1:T(2,128)(2,1)}), bf16[2,128,5120]{2,0,1:T(2,128)(2,1)S(1)}, u32[]{:S(2)}, u32[]{:S(2)}) %all-to-all-start.1) | async-done | bytes 2621472 | tf_op jit(solution)/shard_map/all_to_all | solution.py:66
  414.4 2.9 copy.25
  417.3 4.5 %all_to_all.33 = bf16[2,16,40960]{2,1,0:T(8,128)(2,1)} reshape(bf16[2,16,8,5120]{3,2,1,0:T(8,128)(2,1)} %copy.25) | data formatting | bytes 5242880 | tf_op jit(solution)/shard_map/all_to_all | solution.py:66
  (5 shorter events, 0.1 us)
Async XLA Ops:
  69.2 66.8 %all-to-all-start = ((bf16[8,2,81920]{2,1,0:T(2,128)(2,1)}), bf16[8,2,81920]{2,1,0:T(2,128)(2,1)S(1)}, u32[]{:S(2)}, u32[]{:S(2)}) async-start(bf16[8,2,81920]{2,1,0:T(2,128)(2,1)} %reshape.129), calls=%async_computation | async-start | bytes 5242880 | tf_op jit(solution)/shard_map/all_to_all | solution.py:29
  76.5 226.5 %all-reduce.3.cloned.1.call-start = ((), (), s32[]{:S(2)}) async-start(), calls=%async_computation.2 | async-start | bytes 2621440 | tf_op jit(solution)/shard_map/psum | solution.py:48
  191.2 28.9 %copy-start.1 = (s32[160]{0:T(256)S(1)}, s32[160]{0:T(256)}, u32[]{:S(2)}) copy-start(s32[160]{0:T(256)} %param.8) | copy-start | bytes 1924
  191.2 29.4 %copy-start = (f32[1280,18]{0,1:T(8,128)S(1)}, f32[1280,18]{0,1:T(8,128)}, u32[]{:S(2)}) copy-start(f32[1280,18]{0,1:T(8,128)} %param.7) | copy-start | bytes 276484
  351.2 63.2 %all-to-all-start.1 = ((bf16[2,128,5120]{2,0,1:T(2,128)(2,1)}), bf16[2,128,5120]{2,0,1:T(2,128)(2,1)S(1)}, u32[]{:S(2)}, u32[]{:S(2)}) async-start(bf16[2,128,5120]{2,0,1:T(2,128)(2,1)} %copy.24), calls=%async_computation.1 | async-start | bytes 5242880 | tf_op jit(solution)/shard_map/all_to_all | solution.py:66
Sparse Core Ops, SparseCore 0:
  220.2 82.7 all-reduce.2
where the time goes:
time: 438 us; the launch traced here: 430 us
  waiting for transfers between devices  162 us (37%)
  local copies, waits for them, and re-layouts  156 us (36%)
  matrix products  71.6 us (16%)
  between operations  17 us (4%)
  starting transfers between devices  11.2 us (3%)
  blocking collectives  7.34 us (2%)
  other arithmetic  4.94 us (1%)
    unnamed x8, local copies, waits for them, and re-layouts  103 us
    psum x1, waiting for transfers between devices, shards(): projections = lax.psum(local_terms, 'ga')  81.7 us
    all_to_all x1, waiting for transfers between devices, shards(): lax.all_to_all(result, 'ga', split_axis=1, concat_axis=2, tiled=True)  45.7 us
    all_to_all x1, local copies, waits for them, and re-layouts, shards(): lax.all_to_all(coeffs, 'ga', split_axis=2, concat_axis=1, tiled=True)  37.5 us
    all_to_all x1, waiting for transfers between devices, shards(): lax.all_to_all(coeffs, 'ga', split_axis=2, concat_axis=1, tiled=True)  34.8 us
    dot_general x1, matrix products, shards(): jnp.dot(matrix, projections, precision=lax.Precision.HIGHEST, preferred_e...  29.8 us
    dot_general x1, matrix products, shards(): lax.dot_general(flat_beta, stacked, contract_last, preferred_element_type...  28.8 us
    dot_general x1, matrix products, shards(): lax.dot_general(coupled.astype(jnp.bfloat16), flat_beta, contract_first,...  13 us
  transfers between devices with their start and end apart: 3, of which 3 were waited for; matrix products, arithmetic and copies ran while one was open for 7% of the time, Pallas kernels for 0%

commit v1 on v0

v1 whole, which is shorter than its diff:
```python
import functools
import math

import jax
import jax.numpy as jnp
from jax import lax
from jax.experimental import pallas as pl
from jax.experimental.pallas import tpu as pltpu
from jax.sharding import PartitionSpec as P

MESH = pl.DeviceIdType.MESH
PIECES = 4
STAGE = 128
ROWS = 512


def divisor(total, most, unit):
    size = min(most, total)
    while total % size or size % unit:
        size -= unit
    return size


def diagonals(block_coupling, atom_counts):
    rows, most = block_coupling.shape
    atoms = atom_counts.shape[0]
    earlier = lax.iota(jnp.int32, atoms)[None, :] < lax.iota(jnp.int32, atoms)[:, None]
    starts = jnp.sum(jnp.where(earlier, atom_counts[None, :], 0), axis=1)
    ids = lax.iota(jnp.int32, rows)
    inside = (starts[:, None] <= ids[None, :]) & ((starts + atom_counts)[:, None] > ids[None, :])
    first = jnp.sum(jnp.where(inside, starts[:, None], 0), axis=0)
    length = jnp.sum(jnp.where(inside, atom_counts[:, None], 0), axis=0)
    place = ids - first
    shift = lax.broadcasted_iota(jnp.int32, (2 * most - 1, rows), 0) - (most - 1)
    column = shift + place[None, :]
    fits = column < length[None, :]
    table = jnp.zeros((2 * most - 1, rows), jnp.float32)
    for k in range(most):
        table = jnp.where(fits & (column == k), block_coupling[:, k][None, :], table)
    return jnp.repeat(table, 2, axis=1)


def swap_pairs(values, even_sign, odd_sign):
    lanes = values.shape[-1]
    even = lax.rem(lax.broadcasted_iota(jnp.int32, values.shape, values.ndim - 1), 2) == 0
    up = pltpu.roll(values, lanes - 1, values.ndim - 1)
    down = pltpu.roll(values, 1, values.ndim - 1)
    return jnp.where(even, even_sign * up, odd_sign * down)


def kernel(
    n, nb, counts, coeffs, beta, table, out, energy, total,
    stage, held, xbuf, xt, acc, usend, urecv, dsend, drecv, dfull, obuf,
    esend, erecv, gsend, grecv,
    stage_sem, own_sem, xs, xr, us, ur, ds_, dr, os_, or_, es, er, gs, gr, oown,
):
    me = lax.axis_index("ga")
    mb = lax.axis_index("band")
    own = coeffs.shape[1]
    slots = beta.shape[2]
    rows = held.shape[0]
    bands = n * own
    piece = slots // PIECES
    order = sorted(range(1, n), key=lambda t: -min(t, n - t))
    peers = [lax.rem(me + t, n) for t in order]
    mates = [lax.rem(mb + t, nb) for t in range(1, nb)]

    def stage_copy(i, slot):
        return pltpu.make_async_copy(
            beta.at[pl.ds(i * STAGE, STAGE)], stage.at[slot], stage_sem.at[slot]
        )

    def own_x(c):
        return pltpu.make_async_copy(
            coeffs.at[:, :, pl.ds(pl.multiple_of(me * slots + c * piece, 128), piece)],
            xbuf.at[c, :, me],
            own_sem.at[c],
        )

    def x_copy(c, j, source):
        return pltpu.make_async_remote_copy(
            src_ref=coeffs.at[:, :, pl.ds(pl.multiple_of(j * slots + c * piece, 128), piece)],
            dst_ref=xbuf.at[c, :, source],
            send_sem=xs.at[c, j],
            recv_sem=xr.at[c, source],
            device_id={"ga": j},
            device_id_type=MESH,
        )

    def u_copy(j, source):
        return pltpu.make_async_remote_copy(
            src_ref=usend.at[j], dst_ref=urecv.at[source],
            send_sem=us.at[j], recv_sem=ur.at[source],
            device_id={"ga": j}, device_id_type=MESH,
        )

    def d_copy(j, source):
        return pltpu.make_async_remote_copy(
            src_ref=dsend, dst_ref=drecv.at[source],
            send_sem=ds_.at[j], recv_sem=dr.at[source],
            device_id={"ga": j}, device_id_type=MESH,
        )

    def e_copy(j, source):
        return pltpu.make_async_remote_copy(
            src_ref=esend, dst_ref=erecv.at[source],
            send_sem=es.at[j], recv_sem=er.at[source],
            device_id={"ga": j}, device_id_type=MESH,
        )

    def g_copy(j, source):
        return pltpu.make_async_remote_copy(
            src_ref=gsend, dst_ref=grecv.at[source],
            send_sem=gs.at[j], recv_sem=gr.at[source],
            device_id={"band": j}, device_id_type=MESH,
        )

    def o_copy(c, j, source):
        return pltpu.make_async_remote_copy(
            src_ref=obuf.at[c, :, j],
            dst_ref=out.at[:, :, pl.ds(pl.multiple_of(source * slots + c * piece, 128), piece)],
            send_sem=os_.at[c, j],
            recv_sem=or_.at[c, source],
            device_id={"ga": j},
            device_id_type=MESH,
        )

    def own_o(c):
        return pltpu.make_async_copy(
            obuf.at[c, :, me],
            out.at[:, :, pl.ds(pl.multiple_of(me * slots + c * piece, 128), piece)],
            oown.at[c],
        )

    stage_copy(0, 0).start()
    barrier = pltpu.get_barrier_semaphore()
    for j in peers:
        pl.semaphore_signal(barrier, inc=1, device_id={"ga": j}, device_id_type=MESH)
    for j in mates:
        pl.semaphore_signal(barrier, inc=1, device_id={"band": j}, device_id_type=MESH)
    pl.semaphore_wait(barrier, n - 1 + nb - 1)

    for c in range(PIECES):
        for j in peers:
            x_copy(c, j, me).start()
    for c in range(PIECES):
        own_x(c).start()

    blocks = beta.shape[0] // STAGE
    width = divisor(slots, 512, 128)

    def lay(i, carry):
        slot = lax.rem(i, 2)

        @pl.when(i + 1 < blocks)
        def _():
            stage_copy(i + 1, 1 - slot).start()

        stage_copy(i, slot).wait()

        def cols(w, carry):
            at = pl.ds(pl.multiple_of(w * width, 128), width)
            held[pl.ds(pl.multiple_of(i * 2 * STAGE, 2 * STAGE), 2 * STAGE), at] = stage[
                slot, :, :, at
            ].reshape(2 * STAGE, width)
            return carry

        return lax.fori_loop(0, slots // width, cols, carry)

    lax.fori_loop(0, blocks, lay, 0)

    count = counts[0]
    for c in range(PIECES):
        own_x(c).wait()
        for j in peers:
            x_copy(c, j, j).wait_recv()
        slot_ids = c * piece + lax.broadcasted_iota(jnp.int32, (2 * bands, piece), 1)
        block = xbuf[c].reshape(2 * bands, piece).astype(jnp.float32)
        xt[...] = jnp.where(slot_ids < count, block, 0.0).T.astype(jnp.bfloat16)

        def product(r, carry, c=c):
            at = pl.ds(pl.multiple_of(r * ROWS, ROWS), ROWS)
            term = jnp.dot(
                held[at, c * piece : (c + 1) * piece], xt[...], preferred_element_type=jnp.float32
            )
            if c > 0:
                term = term + acc[at, :]
            if c < PIECES - 1:
                acc[at, :] = term
            else:
                turned = term.T
                united = turned[:bands] + swap_pairs(turned[bands:], 1.0, -1.0)
                usend[:, :, at] = united.astype(jnp.bfloat16).reshape(n, own, ROWS)
            return carry

        lax.fori_loop(0, rows // ROWS, product, 0)

    for j in peers:
        u_copy(j, me).start()
    summed = usend[me].astype(jnp.float32)
    for j in peers:
        u_copy(j, j).wait_recv()
        summed = summed + urecv[j].astype(jnp.float32)
    most = (table.shape[0] + 1) // 2
    coupled = summed * table[most - 1 : most, :]
    for d in range(1 - most, most):
        if d:
            moved = pltpu.roll(summed, (-2 * d) % rows, 1)
            coupled = coupled + moved * table[most - 1 + d : most + d, :]
    dsend[...] = coupled.astype(jnp.bfloat16)
    for j in peers:
        d_copy(j, me).start()
    drecv[me] = coupled.astype(jnp.bfloat16)
    band_energy = jnp.sum(summed * coupled, axis=1, keepdims=True) / beta.shape[0]
    energy[...] = jnp.broadcast_to(band_energy, energy.shape)
    esend[...] = jnp.broadcast_to(jnp.sum(band_energy, axis=0, keepdims=True), esend.shape)
    for j in peers:
        e_copy(j, me).start()

    for j in peers:
        d_copy(j, j).wait_recv()
    real = drecv[...].reshape(bands, rows).astype(jnp.float32)
    dfull[:bands, :] = real.astype(jnp.bfloat16)
    dfull[bands:, :] = swap_pairs(real, -1.0, 1.0).astype(jnp.bfloat16)

    step = divisor(piece, 256, 128)
    for c in range(PIECES):

        def apply(w, carry, c=c):
            lanes = pl.ds(pl.multiple_of(w * step, 128), step)
            slab = pl.ds(pl.multiple_of(c * piece + w * step, 128), step)
            result = jnp.dot(dfull[...], held[:, slab], preferred_element_type=jnp.float32)
            ids = c * piece + w * step + lax.broadcasted_iota(jnp.int32, result.shape, 1)
            result = jnp.where(ids < count, result, 0.0).astype(jnp.bfloat16)
            obuf[c, :, :, :, lanes] = result.reshape(2, n, own, step)
            return carry

        lax.fori_loop(0, piece // step, apply, 0)
        for j in peers:
            o_copy(c, j, me).start()
        own_o(c).start()

    group = esend[...]
    for j in peers:
        e_copy(j, j).wait_recv()
        group = group + erecv[j]
    gsend[...] = group
    for j in mates:
        g_copy(j, mb).start()
    whole = group
    for j in mates:
        g_copy(j, j).wait_recv()
        whole = whole + grecv[j]
    total[...] = whole / math.sqrt(n * nb * own)

    for c in range(PIECES):
        for j in peers:
            x_copy(c, j, me).wait_send()
            o_copy(c, j, me).wait_send()
            o_copy(c, j, j).wait_recv()
        own_o(c).wait()
    for j in peers:
        u_copy(j, me).wait_send()
        d_copy(j, me).wait_send()
        e_copy(j, me).wait_send()
    for j in mates:
        g_copy(j, mb).wait_send()


def shards(n, nb, coeffs, projectors, block_coupling, atom_counts, wave_counts):
    own = coeffs.shape[1]
    count, _, slots = projectors.shape
    rows = 2 * count
    bands = n * own
    piece = slots // PIECES
    low, full = jnp.bfloat16, jnp.float32
    dma = pltpu.SemaphoreType.DMA
    table = diagonals(block_coupling, atom_counts)
    flops = 4 * rows * slots * 2 * bands
    out, energy, total = pl.pallas_call(
        functools.partial(kernel, n, nb),
        out_shape=(
            jax.ShapeDtypeStruct(coeffs.shape, low),
            jax.ShapeDtypeStruct((own, 128), full),
            jax.ShapeDtypeStruct((8, 128), full),
        ),
        in_specs=[
            pl.BlockSpec(memory_space=pltpu.SMEM),
            pl.BlockSpec(memory_space=pl.ANY),
            pl.BlockSpec(memory_space=pl.ANY),
            pl.BlockSpec(memory_space=pltpu.VMEM),
        ],
        out_specs=(
            pl.BlockSpec(memory_space=pl.ANY),
            pl.BlockSpec(memory_space=pltpu.VMEM),
            pl.BlockSpec(memory_space=pltpu.VMEM),
        ),
        scratch_shapes=[
            pltpu.VMEM((2, STAGE, 2, slots), low),
            pltpu.VMEM((rows, slots), low),
            pltpu.VMEM((PIECES, 2, n, own, piece), low),
            pltpu.VMEM((piece, 2 * bands), low),
            pltpu.VMEM((rows, 2 * bands), full),
            pltpu.VMEM((n, own, rows), low),
            pltpu.VMEM((n, own, rows), low),
            pltpu.VMEM((own, rows), low),
            pltpu.VMEM((n, own, rows), low),
            pltpu.VMEM((2 * bands, rows), low),
            pltpu.VMEM((PIECES, 2, n, own, piece), low),
            pltpu.VMEM((8, 128), full),
            pltpu.VMEM((n, 8, 128), full),
            pltpu.VMEM((8, 128), full),
            pltpu.VMEM((nb, 8, 128), full),
            dma((2,)),
            dma((PIECES,)),
            dma((PIECES, n)),
            dma((PIECES, n)),
            dma((n,)),
            dma((n,)),
            dma((n,)),
            dma((n,)),
            dma((PIECES, n)),
            dma((PIECES, n)),
            dma((n,)),
            dma((n,)),
            dma((nb,)),
            dma((nb,)),
            dma((PIECES,)),
        ],
        compiler_params=pltpu.CompilerParams(
            collective_id=0, has_side_effects=True, vmem_limit_bytes=62 * 2**20
        ),
        cost_estimate=pl.CostEstimate(
            flops=flops, bytes_accessed=2 * rows * slots, transcendentals=0
        ),
    )(wave_counts, coeffs, projectors, table)
    return (out, energy[:, 0], total[0, 0])


def solution(mesh):
    placed = (P(None, ("ga", "band"), None), P(None, None, "ga"), P(), P(), P("ga"))
    return jax.shard_map(
        functools.partial(shards, mesh.shape["ga"], mesh.shape["band"]),
        mesh=mesh,
        in_specs=placed,
        out_specs=(P(None, ("ga", "band"), None), P(("ga", "band")), P()),
        check_vma=False,
    )
```

time: 438 us -> 174 us (0.40); the launches traced: 430 us -> 171 us
  waiting for transfers between devices: 162 us -> 0 us
  Pallas kernels: 0 us -> 154 us
  local copies, waits for them, and re-layouts: 156 us -> 9.29 us
  matrix products: 71.6 us -> 0 us
  between operations: 17 us -> 1.33 us
  starting transfers between devices: 11.2 us -> 0 us
  blocking collectives: 7.34 us -> 0 us
    pallas_call x0 -> x1, Pallas kernels: none -> 154 us  [shards(): pl.pallas_call(functools.partial(kernel, n, nb), out_shape=(jax.ShapeDtyp...]
    unnamed x8 -> x1, local copies, waits for them, and re-layouts: 103 us -> 3.4 us
    psum x1 -> x0, waiting for transfers between devices: 81.7 us -> none  [shards(): projections = lax.psum(local_terms, 'ga')]
    all_to_all x2 -> x0, waiting for transfers between devices: 80.5 us -> none  [the longest x1 45.7 us: shards(): lax.all_to_all(result, 'ga', split_axis=1, concat_axis=2, tiled=True)]
    dot_general x3 -> x0, matrix products: 71.6 us -> none  [the longest x1 29.8 us: shards(): jnp.dot(matrix, projections, precision=lax.Precision.HIGHEST, preferred_e...]
    all_to_all x3 -> x0, local copies, waits for them, and re-layouts: 44.9 us -> none  [the longest x1 37.5 us: shards(): lax.all_to_all(coeffs, 'ga', split_axis=2, concat_axis=1, tiled=True)]
    all_to_all x2 -> x0, starting transfers between devices: 10.9 us -> none  [the longest x1 7.28 us: shards(): lax.all_to_all(coeffs, 'ga', split_axis=2, concat_axis=1, tiled=True)]
    psum x1 -> x0, blocking collectives: 7.34 us -> none  [shards(): total_energy = lax.psum(jnp.sum(group_energy), 'band')]
  transfers between devices with their start and end apart: 3 -> 0, of which waited for: 3 -> 0; matrix products, arithmetic and copies ran while one was open for 7% -> 0% of each run, Pallas kernels for 0% -> 0%
where the time goes in v1:
time: 174 us; the launch traced here: 171 us
  Pallas kernels  154 us (89%)
  local copies, waits for them, and re-layouts  9.29 us (5%)
  other arithmetic  6.05 us (3%)
    pallas_call x1, Pallas kernels, shards(): pl.pallas_call(functools.partial(kernel, n, nb), out_shape=(jax.ShapeDtyp...  154 us
    select_n x1, other arithmetic, diagonals(): jnp.where(fits & (column == k), block_coupling[:, k][None, :], table)  3.57 us

profile of v1, /device:TPU:0, one launch (start us, length us, event | category | flops | bytes accessed | tf_op | source)
XLA Modules:
  0.0 170.9 jit_solution(2457671874752116246)
XLA Ops:
  1.3 0.8 select_reduce_fusion.2
  2.1 0.7 add.13
  2.8 1.0 select_reduce_fusion.1
  3.8 1.7 %slice_reduce_fusion.18 = (f32[1280]{0:T(1024)S(1)}, f32[1280]{0:T(1024)S(1)}, f32[1280]{0:T(1024)S(1)}, f32[1280]{0:T(1024)S(1)}, f32[1280]{0:T(1024)S(1)}, /*i...) fusion(f32[1280,18]{0,1:T(8,128)} %param.7), kind=kLoop, calls=%fused_computation.64 | loop fusion | bytes 184320 | tf_op jit(solution)/shard_map/slice | solution.py:39
  5.5 3.6 %select_select_fusion = f32[35,1280]{0,1:T(8,128)S(1)} fusion(f32[1280]{0:T(1024)S(1)} %get-tuple-element.25, f32[1280]{0:T(1024)S(1)} %get-tuple-element.26, f32[1280]{0:T(1024)S(1)} %get-tuple-element.10, f32[1280]{0:T(1024)S(1)} %get-tuple-element.11, f32[1280]{0:T(1024)S(1)} %get-tuple-element.12, f32[1280]{0:T(1024)S(1)} %get-tuple-element.13, ...), kind=kLoop, calls=%fused_computation.42 | loop fusion | flops 2508800 | bytes 281740 | tf_op jit(solution)/shard_map/jit(_where)/select_n | solution.py:39
  9.1 0.5 broadcast_in_dim.215
  9.6 1.2 copy.9.table
  10.7 154.3 %shard_map.76 = (bf16[2,16,40960]{2,1,0:T(8,128)(2,1)}, f32[16,128]{1,0:T(8,128)}, f32[8,128]{1,0:T(8,128)}) custom-call(s32[1]{0:T(128)S(6)} %copy.11.counts, bf16[2,16,40960]{2,1,0:T(8,128)(2,1)} %coeffs.1, bf16[1280,2,5120]{2,1,0:T(2,128)(2,1)} %beta.1, f32[35,2560]{1,0:T(8,128)} %copy.9.table), custom_call_target="tpu_custom_call" | custom-call | flops 13421772800 | bytes 26214400 | tf_op jit(solution)/shard_map/pallas_call | solution.py:280
  165.0 1.2 slice.79
  166.2 1.3 slice_reduce_fusion
  167.5 3.4 %copy.12 = bf16[2,16,40960]{2,1,0:T(8,128)(2,1)} copy(bf16[2,16,40960]{2,1,0:T(8,128)(2,1)} %get-tuple-element.32) | data formatting | bytes 5242880
  (2 shorter events, 0.0 us)

commit v2 on v1

v2 whole, which is shorter than its diff:
```python
import functools
import math

import jax
import jax.numpy as jnp
from jax import lax
from jax.experimental import pallas as pl
from jax.experimental.pallas import tpu as pltpu
from jax.sharding import PartitionSpec as P

MESH = pl.DeviceIdType.MESH
HALVES = 2
PIECES = 4
STAGE = 128
ROWS = 512


def divisor(total, most, unit):
    size = min(most, total)
    while total % size or size % unit:
        size -= unit
    return size


def diagonals(counts, coupling):
    atoms = counts.shape[1]
    most, rows = coupling.shape
    counts = counts.astype(jnp.float32)
    square = (atoms, atoms)
    across = lax.broadcasted_iota(jnp.int32, square, 1)
    down = lax.broadcasted_iota(jnp.int32, square, 0)
    starts = jnp.sum(jnp.where(across < down, counts, 0.0), axis=1, keepdims=True)
    sizes = jnp.sum(jnp.where(across == down, counts, 0.0), axis=1, keepdims=True)
    ids = lax.broadcasted_iota(jnp.int32, (atoms, rows), 1).astype(jnp.float32)
    inside = (starts <= ids) & (ids < starts + sizes)
    first = jnp.sum(jnp.where(inside, starts, 0.0), axis=0, keepdims=True)
    length = jnp.sum(jnp.where(inside, sizes, 0.0), axis=0, keepdims=True)
    shape = (2 * most - 1, rows)
    shift = lax.broadcasted_iota(jnp.int32, shape, 0) - (most - 1)
    place = lax.broadcasted_iota(jnp.int32, shape, 1) - first.astype(jnp.int32)
    column = shift + place
    fits = column < length.astype(jnp.int32)
    table = jnp.zeros(shape, jnp.float32)
    for k in range(most):
        table = jnp.where(fits & (column == k), coupling[k : k + 1, :], table)
    unit = divisor(rows, 128, 128)
    wide = lax.broadcasted_iota(jnp.int32, (unit, 2 * unit), 1)
    source = lax.broadcasted_iota(jnp.int32, (unit, 2 * unit), 0)
    twice = ((wide == 2 * source) | (wide == 2 * source + 1)).astype(jnp.float32)
    return [
        jnp.dot(
            table[:, at : at + unit],
            twice,
            precision=lax.Precision.HIGHEST,
            preferred_element_type=jnp.float32,
        )
        for at in range(0, rows, unit)
    ]


def swap_pairs(values, even_sign, odd_sign):
    lanes = values.shape[-1]
    even = lax.rem(lax.broadcasted_iota(jnp.int32, values.shape, values.ndim - 1), 2) == 0
    up = pltpu.roll(values, lanes - 1, values.ndim - 1)
    down = pltpu.roll(values, 1, values.ndim - 1)
    return jnp.where(even, even_sign * up, odd_sign * down)


def kernel(
    n, nb, counts, coeffs, beta, coupling, atoms, out, energy, total,
    stage, held, xbuf, xt, acc, table, usend, urecv, usum, csend, crecv, dsend, drecv, dfull,
    obuf, esend, erecv, gsend, grecv,
    stage_sem, own_sem, xs, xr, us, ur, cs, cr, ds_, fs, bs, dr, os_, or_, es, er, gs, gr, oown,
):
    me = lax.axis_index("ga")
    mb = lax.axis_index("band")
    slots = beta.shape[2]
    rows = held.shape[0]
    own = coeffs.shape[1]
    part = own // HALVES
    bands = n * part
    piece = slots // PIECES
    near = n // 2
    side, spot = me // near, lax.rem(me, near)
    other = lax.rem(me + near, n)
    order = sorted(range(1, n), key=lambda t: -min(t, n - t))
    peers = [lax.rem(me + t, n) for t in order]
    mates = [lax.rem(mb + t, nb) for t in range(1, nb)]
    spots = [lax.rem(spot + t, near) for t in range(1, near)]

    def remote(src, dst, send, recv, j, axis="ga"):
        return pltpu.make_async_remote_copy(
            src_ref=src, dst_ref=dst, send_sem=send, recv_sem=recv,
            device_id={axis: j}, device_id_type=MESH,
        )

    def stage_copy(i, slot):
        return pltpu.make_async_copy(
            beta.at[pl.ds(i * STAGE, STAGE)], stage.at[slot], stage_sem.at[slot]
        )

    def x_part(h, c, j):
        at = pl.ds(pl.multiple_of(j * slots + c * piece, 128), piece)
        return coeffs.at[:, h * part : (h + 1) * part, at]

    def o_part(h, c, j):
        at = pl.ds(pl.multiple_of(j * slots + c * piece, 128), piece)
        return out.at[:, h * part : (h + 1) * part, at]

    def own_x(h, c):
        return pltpu.make_async_copy(x_part(h, c, me), xbuf.at[h, c, :, me], own_sem.at[h, c])

    def x_copy(h, c, j, source):
        return remote(
            x_part(h, c, j), xbuf.at[h, c, :, source], xs.at[h, c, j], xr.at[h, c, source], j
        )

    def own_o(h, c):
        return pltpu.make_async_copy(obuf.at[h, c, :, me], o_part(h, c, me), oown.at[h, c])

    def o_copy(h, c, j, source):
        return remote(
            obuf.at[h, c, :, j], o_part(h, c, source), os_.at[h, c, j], or_.at[h, c, source], j
        )

    def u_copy(h, at, source):
        return remote(
            usend.at[h, :, at], urecv.at[h, source], us.at[h, at], ur.at[h, source],
            side * near + at,
        )

    def c_copy(h):
        return remote(csend.at[h], crecv.at[h], cs.at[h], cr.at[h], other)

    def d_copy(h, at, source):
        return remote(
            dsend.at[h], drecv.at[h, side * near + source], ds_.at[h, at],
            dr.at[h, side * near + source], side * near + at,
        )

    def b_copy(h, source):
        return remote(dsend.at[h], drecv.at[h, source], bs.at[h], dr.at[h, source], other)

    def f_copy(h, at, source):
        block = drecv.at[h, (1 - side) * near + source]
        return remote(
            block, block, fs.at[h, at], dr.at[h, (1 - side) * near + source], side * near + at
        )

    def e_copy(j, source):
        return remote(esend, erecv.at[source], es.at[j], er.at[source], j)

    def g_copy(j, source):
        return remote(gsend, grecv.at[source], gs.at[j], gr.at[source], j, "band")

    def send_x(h, c):
        for j in peers:
            x_copy(h, c, j, me).start()

    count = counts[0]

    def first_product(h, c):
        own_x(h, c).wait()
        for j in peers:
            x_copy(h, c, j, j).wait_recv()
        slot_ids = c * piece + lax.broadcasted_iota(jnp.int32, (2 * bands, piece), 1)
        block = xbuf[h, c].astype(jnp.float32).reshape(2 * bands, piece)
        xt[...] = jnp.where(slot_ids < count, block, 0.0).T.astype(jnp.bfloat16)

        def product(r, carry):
            at = pl.ds(pl.multiple_of(r * ROWS, ROWS), ROWS)
            term = jnp.dot(
                held[at, c * piece : (c + 1) * piece], xt[...], preferred_element_type=jnp.float32
            )
            if c > 0:
                term = term + acc[at, :]
            if c < PIECES - 1:
                acc[at, :] = term
            else:
                turned = term.T
                united = turned[:bands] + swap_pairs(turned[bands:], 1.0, -1.0)
                united = united.reshape(2, near, part, ROWS)
                usend[h, :, :, :, at] = united.astype(jnp.bfloat16)
            return carry

        lax.fori_loop(0, rows // ROWS, product, 0)

    def send_sums(h):
        for at in spots:
            u_copy(h, at, spot).start()

    def half_sums(h):
        same = usend[h, side, spot].astype(jnp.float32)
        away = usend[h, 1 - side, spot].astype(jnp.float32)
        for at in spots:
            u_copy(h, at, at).wait_recv()
            same = same + urecv[h, at, side].astype(jnp.float32)
            away = away + urecv[h, at, 1 - side].astype(jnp.float32)
        csend[h] = away.astype(jnp.bfloat16)
        c_copy(h).start()
        usum[h] = same

    def couple(h):
        c_copy(h).wait_recv()
        summed = usum[h] + crecv[h].astype(jnp.float32)
        most = (table.shape[0] + 1) // 2
        coupled = summed * table[most - 1 : most, :]
        for d in range(1 - most, most):
            if d:
                moved = pltpu.roll(summed, (-2 * d) % rows, 1)
                coupled = coupled + moved * table[most - 1 + d : most + d, :]
        low = coupled.astype(jnp.bfloat16)
        dsend[h] = low
        b_copy(h, me).start()
        for at in spots:
            d_copy(h, at, spot).start()
        drecv[h, me] = low
        bands_now = jnp.sum(summed * coupled, axis=1, keepdims=True) / beta.shape[0]
        lanes = lax.broadcasted_iota(jnp.int32, (part, own), 1)
        line = lax.broadcasted_iota(jnp.int32, (part, own), 0) + h * part
        row = jnp.sum(jnp.where(lanes == line, bands_now, 0.0), axis=0, keepdims=True)
        sofar = jnp.broadcast_to(jnp.sum(bands_now, axis=0, keepdims=True), esend.shape)
        if h == 0:
            energy[...] = row
            gsend[...] = sofar
        else:
            energy[...] = energy[...] + row
            esend[...] = gsend[...] + sofar
            for j in peers:
                e_copy(j, me).start()

    def pass_on(h):
        b_copy(h, other).wait_recv()
        for at in spots:
            f_copy(h, at, spot).start()

    def gather(h):
        for at in spots:
            d_copy(h, at, at).wait_recv()
            f_copy(h, at, at).wait_recv()
        real = drecv[h].astype(jnp.float32).reshape(bands, rows)
        dfull[:bands, :] = real.astype(jnp.bfloat16)
        dfull[bands:, :] = swap_pairs(real, -1.0, 1.0).astype(jnp.bfloat16)

    step = divisor(piece, 256, 128)

    def second_product(h, c):
        def apply(w, carry):
            lanes = pl.ds(pl.multiple_of(w * step, 128), step)
            slab = pl.ds(pl.multiple_of(c * piece + w * step, 128), step)
            result = jnp.dot(dfull[...], held[:, slab], preferred_element_type=jnp.float32)
            ids = c * piece + w * step + lax.broadcasted_iota(jnp.int32, result.shape, 1)
            result = jnp.where(ids < count, result, 0.0).reshape(2, n, part, step)
            obuf[h, c, :, :, :, lanes] = result.astype(jnp.bfloat16)
            return carry

        lax.fori_loop(0, piece // step, apply, 0)
        for j in peers:
            o_copy(h, c, j, me).start()
        own_o(h, c).start()

    stage_copy(0, 0).start()
    barrier = pltpu.get_barrier_semaphore()
    for j in peers:
        pl.semaphore_signal(barrier, inc=1, device_id={"ga": j}, device_id_type=MESH)
    for j in mates:
        pl.semaphore_signal(barrier, inc=1, device_id={"band": j}, device_id_type=MESH)
    pl.semaphore_wait(barrier, n - 1 + nb - 1)

    for c in range(PIECES):
        send_x(0, c)
    early = PIECES // 2
    for c in range(early):
        send_x(1, c)
    for h in range(HALVES):
        for c in range(PIECES):
            own_x(h, c).start()

    blocks = beta.shape[0] // STAGE
    width = divisor(slots, 512, 128)

    def lay(i, carry):
        slot = lax.rem(i, 2)

        @pl.when(i + 1 < blocks)
        def _():
            stage_copy(i + 1, 1 - slot).start()

        stage_copy(i, slot).wait()

        def cols(w, carry):
            at = pl.ds(pl.multiple_of(w * width, 128), width)
            held[pl.ds(pl.multiple_of(i * 2 * STAGE, 2 * STAGE), 2 * STAGE), at] = stage[
                slot, :, :, at
            ].reshape(2 * STAGE, width)
            return carry

        return lax.fori_loop(0, slots // width, cols, carry)

    lax.fori_loop(0, blocks, lay, 0)
    strips = diagonals(atoms[...], coupling[...])
    wide = rows // len(strips)
    for i, strip in enumerate(strips):
        table[:, i * wide : (i + 1) * wide] = strip

    for c in range(PIECES):
        first_product(0, c)
    send_sums(0)
    for c in range(early, PIECES - 1):
        send_x(1, c)
    first_product(1, 0)
    half_sums(0)
    send_x(1, PIECES - 1)
    first_product(1, 1)
    couple(0)
    for c in range(2, PIECES - 1):
        first_product(1, c)
    pass_on(0)
    first_product(1, PIECES - 1)
    send_sums(1)
    gather(0)
    second_product(0, 0)
    half_sums(1)
    second_product(0, 1)
    couple(1)
    for c in range(2, PIECES - 1):
        second_product(0, c)
    pass_on(1)
    second_product(0, PIECES - 1)
    gather(1)
    for c in range(PIECES):
        second_product(1, c)

    for j in peers:
        e_copy(j, me).wait_send()
    group = esend[...]
    for j in peers:
        e_copy(j, j).wait_recv()
        group = group + erecv[j]
    gsend[...] = group
    for j in mates:
        g_copy(j, mb).start()
    whole = group
    for j in mates:
        g_copy(j, j).wait_recv()
        whole = whole + grecv[j]
    total[...] = whole[:1, :1] / math.sqrt(n * nb * own)

    for j in mates:
        g_copy(j, mb).wait_send()
    for h in range(HALVES):
        for c in range(PIECES):
            for j in peers:
                x_copy(h, c, j, me).wait_send()
                o_copy(h, c, j, me).wait_send()
                o_copy(h, c, j, j).wait_recv()
            own_o(h, c).wait()
        for at in spots:
            u_copy(h, at, spot).wait_send()
            d_copy(h, at, spot).wait_send()
            f_copy(h, at, spot).wait_send()
        c_copy(h).wait_send()
        b_copy(h, me).wait_send()


def shards(n, nb, coeffs, projectors, block_coupling, atom_counts, wave_counts):
    own = coeffs.shape[1]
    count, _, slots = projectors.shape
    most = block_coupling.shape[1]
    rows = 2 * count
    part = own // HALVES
    bands = n * part
    near = n // 2
    piece = slots // PIECES
    low, full = jnp.bfloat16, jnp.float32
    dma = pltpu.SemaphoreType.DMA
    out, energy, total = pl.pallas_call(
        functools.partial(kernel, n, nb),
        out_shape=(
            jax.ShapeDtypeStruct(coeffs.shape, low),
            jax.ShapeDtypeStruct((1, own), full),
            jax.ShapeDtypeStruct((1, 1), full),
        ),
        in_specs=[
            pl.BlockSpec(memory_space=pltpu.SMEM),
            pl.BlockSpec(memory_space=pl.ANY),
            pl.BlockSpec(memory_space=pl.ANY),
            pl.BlockSpec(memory_space=pltpu.VMEM),
            pl.BlockSpec(memory_space=pltpu.VMEM),
        ],
        out_specs=(
            pl.BlockSpec(memory_space=pl.ANY),
            pl.BlockSpec(memory_space=pltpu.VMEM),
            pl.BlockSpec(memory_space=pltpu.VMEM),
        ),
        scratch_shapes=[
            pltpu.VMEM((2, STAGE, 2, slots), low),
            pltpu.VMEM((rows, slots), low),
            pltpu.VMEM((HALVES, PIECES, 2, n, part, piece), low),
            pltpu.VMEM((piece, 2 * bands), low),
            pltpu.VMEM((rows, 2 * bands), full),
            pltpu.VMEM((2 * most - 1, rows), full),
            pltpu.VMEM((HALVES, 2, near, part, rows), low),
            pltpu.VMEM((HALVES, near, 2, part, rows), low),
            pltpu.VMEM((HALVES, part, rows), full),
            pltpu.VMEM((HALVES, part, rows), low),
            pltpu.VMEM((HALVES, part, rows), low),
            pltpu.VMEM((HALVES, part, rows), low),
            pltpu.VMEM((HALVES, n, part, rows), low),
            pltpu.VMEM((2 * bands, rows), low),
            pltpu.VMEM((HALVES, PIECES, 2, n, part, piece), low),
            pltpu.VMEM((8, 128), full),
            pltpu.VMEM((n, 8, 128), full),
            pltpu.VMEM((8, 128), full),
            pltpu.VMEM((nb, 8, 128), full),
            dma((2,)),
            dma((HALVES, PIECES)),
            dma((HALVES, PIECES, n)),
            dma((HALVES, PIECES, n)),
            dma((HALVES, near)),
            dma((HALVES, near)),
            dma((HALVES,)),
            dma((HALVES,)),
            dma((HALVES, near)),
            dma((HALVES, near)),
            dma((HALVES,)),
            dma((HALVES, n)),
            dma((HALVES, PIECES, n)),
            dma((HALVES, PIECES, n)),
            dma((n,)),
            dma((n,)),
            dma((nb,)),
            dma((nb,)),
            dma((HALVES, PIECES)),
        ],
        compiler_params=pltpu.CompilerParams(
            collective_id=0, has_side_effects=True, vmem_limit_bytes=62 * 2**20
        ),
        cost_estimate=pl.CostEstimate(
            flops=8 * rows * slots * n * own, bytes_accessed=2 * rows * slots, transcendentals=0
        ),
    )(wave_counts, coeffs, projectors, block_coupling.T, atom_counts.reshape(1, -1))
    return (out, energy.reshape(own), total.reshape(()))


def solution(mesh):
    placed = (P(None, ("ga", "band"), None), P(None, None, "ga"), P(), P(), P("ga"))
    return jax.shard_map(
        functools.partial(shards, mesh.shape["ga"], mesh.shape["band"]),
        mesh=mesh,
        in_specs=placed,
        out_specs=(P(None, ("ga", "band"), None), P(("ga", "band")), P()),
        check_vma=False,
    )
```

time: 174 us -> 145 us (0.83); the launches traced: 171 us -> 145 us
  Pallas kernels: 154 us -> 138 us
  other arithmetic: 6.05 us -> 0 us
  local copies, waits for them, and re-layouts: 9.29 us -> 3.92 us
  between operations: 1.33 us -> 3.09 us
    pallas_call x1, Pallas kernels: 154 us -> 138 us  [shards(): pl.pallas_call(functools.partial(kernel, n, nb), out_shape=(jax.ShapeDtyp...]
    slice x3 -> x0, local copies, waits for them, and re-layouts: 4.23 us -> none  [the longest x2 2.51 us: shards(): return (out, energy[:, 0], total[0, 0])]
    select_n x1 -> x0, other arithmetic: 3.57 us -> none  [diagonals(): jnp.where(fits & (column == k), block_coupling[:, k][None, :], table)]
    reduce_sum x2 -> x0, other arithmetic: 1.78 us -> none  [the longest x1 0.99 us: diagonals(): first = jnp.sum(jnp.where(inside, starts[:, None], 0), axis=0)]
    unnamed x1 -> x4, local copies, waits for them, and re-layouts: 3.4 us -> 3.92 us
where the time goes in v2:
time: 145 us
  Pallas kernels  138 us (95%)
  local copies, waits for them, and re-layouts  3.92 us (3%)
  between operations  3.09 us (2%)
    pallas_call x1, Pallas kernels, shards(): pl.pallas_call(functools.partial(kernel, n, nb), out_shape=(jax.ShapeDtyp...  138 us
    unnamed x4, local copies, waits for them, and re-layouts  3.92 us

profile of v2, /device:TPU:0, one launch (start us, length us, event | category | flops | bytes accessed | tf_op | source)
XLA Modules:
  0.0 145.2 jit_solution(17721989601389879703)
XLA Ops:
  1.3 138.2 %shard_map.76 = (bf16[2,16,40960]{2,1,0:T(8,128)(2,1)}, f32[1,16]{1,0:T(1,128)}, f32[1,1]{1,0:T(1,128)}) custom-call(s32[1]{0:T(128)S(6)} %copy.11.counts, bf16[2,16,40960]{2,1,0:T(8,128)(2,1)} %coeffs.1, bf16[1280,2,5120]{2,1,0:T(2,128)(2,1)} %beta.1, f32[18,1280]{1,0:T(8,128)} %bitcast.4, s32[1,160]{1,0:T(1,128)} %bitcast.5), custom_call_target="tpu_custom_call" | custom-call | flops 13421772800 | bytes 26214400 | tf_op jit(solution)/shard_map/pallas_call | solution.py:377
  139.5 0.0 copy-start
  139.5 3.4 %copy.12 = bf16[2,16,40960]{2,1,0:T(8,128)(2,1)} copy(bf16[2,16,40960]{2,1,0:T(8,128)(2,1)} %get-tuple-element.12) | data formatting | bytes 5242880
  142.9 0.0 copy-done
  142.9 0.5 copy.13
Async XLA Ops:
  139.5 3.4 %copy-start = (f32[1,16]{1,0:T(1,128)S(1)}, f32[1,16]{1,0:T(1,128)}, u32[]{:S(2)}) copy-start(f32[1,16]{1,0:T(1,128)} %get-tuple-element.7) | copy-start | bytes 196

commit v3 on v2

--- a/solution.py
+++ b/solution.py
@@ -383,8 +383,8 @@
         ),
         in_specs=[
             pl.BlockSpec(memory_space=pltpu.SMEM),
-            pl.BlockSpec(memory_space=pl.ANY),
-            pl.BlockSpec(memory_space=pl.ANY),
+            pl.BlockSpec(memory_space=pltpu.HBM),
+            pl.BlockSpec(memory_space=pltpu.HBM),
             pl.BlockSpec(memory_space=pltpu.VMEM),
             pl.BlockSpec(memory_space=pltpu.VMEM),
         ],
@@ -434,7 +434,7 @@
             dma((HALVES, PIECES)),
         ],
         compiler_params=pltpu.CompilerParams(
-            collective_id=0, has_side_effects=True, vmem_limit_bytes=62 * 2**20
+            collective_id=0, has_side_effects=True, vmem_limit_bytes=50 * 2**20
         ),
         cost_estimate=pl.CostEstimate(
             flops=8 * rows * slots * n * own, bytes_accessed=2 * rows * slots, transcendentals=0

time: 145 us -> 144 us (level)
    unnamed x4 -> x6, local copies, waits for them, and re-layouts: 3.92 us -> 3.58 us
where the time goes in v3:
time: 144 us
  Pallas kernels  137 us (95%)
  local copies, waits for them, and re-layouts  3.58 us (2%)
  between operations  3.06 us (2%)
    pallas_call x1, Pallas kernels, shards(): pl.pallas_call(functools.partial(kernel, n, nb), out_shape=(jax.ShapeDtyp...  137 us
    unnamed x6, local copies, waits for them, and re-layouts  3.58 us

profile of v3, /device:TPU:0, one launch (start us, length us, event | category | flops | bytes accessed | tf_op | source)
XLA Modules:
  0.0 143.8 jit_solution(1063445470993177597)
XLA Ops:
  1.3 0.0 copy-start
  1.3 0.9 copy-done
  2.2 0.0 copy-start.1
  2.2 0.7 copy-done.1
  2.9 137.1 %shard_map.76 = (bf16[2,16,40960]{2,1,0:T(8,128)(2,1)S(1)}, f32[1,16]{1,0:T(1,128)S(1)}, f32[1,1]{1,0:T(1,128)}) custom-call(s32[1]{0:T(128)S(6)} %copy.11.counts, bf16[2,16,40960]{2,1,0:T(8,128)(2,1)} %coeffs.1, bf16[1280,2,5120]{2,1,0:T(2,128)(2,1)} %beta.1, f32[18,1280]{1,0:T(8,128)S(1)} %bitcast.4, s32[1,160]{1,0:T(1,128)S(1)} %bitcast.5), custom_call_target="tpu_custom_call" | custom-call | flops 13421772800 | bytes 26214400 | tf_op jit(solution)/shard_map/pallas_call | solution.py:377
  140.0 1.5 %copy.12 = bf16[2,16,40960]{2,1,0:T(8,128)(2,1)} copy(bf16[2,16,40960]{2,1,0:T(8,128)(2,1)S(1)} %get-tuple-element.12) | data formatting | bytes 5242880
  141.5 0.5 copy.13
Async XLA Ops:
  1.3 0.9 copy-start
  2.2 0.7 copy-start.1
